TPU v7x, 32 devices: a whole 2x2x4 slice. The times are simulated.
32 devices in a mesh: feat: 8 (over z, x), samp: 4 (over y, core).
Axes of the slice: x: 2, y: 2, z: 4, core: 2. Of those that a mesh axis runs over, the one named last changes fastest.
Arguments:
- tiles: float32 [32, 64, 128, 128], P('feat', 'samp'), may hold values from -0.0625 to 0.0625
- row_index: int32 [32, 64], P('feat', 'samp'), may hold values from 0 to 511
- targets: float32 [2048, 128], P('samp'), may hold values from -15 to 15
- penalty: float32 [32, 128], P('feat'), may hold values from 0.8 to 8
- picks: int32 [3, 16], P(None, 'feat'), may hold values from 0 to 3, as said below
Outputs:
- weights: float32 [32, 128], P('feat')
- residual: float32 [2048, 128], P('samp')
- gaps: float32 [3], replicated
Inputs may be any that keep to these rules, and one draw needn't show every extreme that they name: Within one iteration the 2 entries of one feature group, picks[t, g * 2 : (g + 1) * 2], are distinct local block numbers.
All inputs are finite; a program needn't handle non-finite values.
Results may differ from a plain program's by a relative error of at most 0.0003.
Values sent between devices are 32-bit elements; how exact they have to be, the bound alone decides.
A program may use at most 64 MiB of HBM per device.

v0:
```python
import jax
import jax.numpy as jnp
from jax import lax
from jax.sharding import PartitionSpec as P

ITERS = 3


STEP_SCALE = 2.0
EPSILON = 1e-06


def shards(tiles, row_index, targets, penalty, picks):
    precise = lax.Precision.HIGHEST
    blocks_dev = row_index.shape[0]
    row_blocks = targets.shape[0]
    col_local = jnp.sum(tiles * tiles, axis=(1, 2))
    residual = -targets
    weights = jnp.zeros((blocks_dev, 128), jnp.float32)
    col_sq = None
    base = None
    gap_list = []
    for iteration in range(ITERS):
        fetched = residual[row_index]
        grad_local = jnp.einsum("bkrf,bkr->bf", tiles, fetched, precision=precise)
        rr_local = jnp.sum(residual * residual)
        ry_local = jnp.sum(residual * targets)
        if iteration == 0:
            grad, sum_rr, sum_ry, col_sq = lax.psum(
                (grad_local, rr_local, ry_local, col_local), "samp"
            )
            base = sum_rr
        else:
            grad, sum_rr, sum_ry = lax.psum((grad_local, rr_local, ry_local), "samp")
        ratio_local = jnp.min(penalty / jnp.maximum(jnp.abs(grad), penalty))
        norm_local = jnp.sum(penalty * jnp.abs(weights))
        scale = lax.pmin(ratio_local, "feat")
        norm_one = lax.psum(norm_local, "feat")
        gap_list.append(
            (0.5 * sum_rr + norm_one + 0.5 * scale * scale * sum_rr + scale * sum_ry) / (0.5 * base)
        )
        chosen = picks[iteration]
        pick_hot = (chosen[:, None] == jnp.arange(blocks_dev, dtype=jnp.int32)[None, :]).astype(
            jnp.float32
        )
        stacked = jnp.stack([grad, col_sq, weights, penalty], axis=0)
        selected = jnp.einsum("pb,sbf->spf", pick_hot, stacked, precision=precise)
        denom = STEP_SCALE * (selected[1] + EPSILON)
        moved = selected[2] - selected[0] / denom
        shrunk = jnp.sign(moved) * jnp.maximum(jnp.abs(moved) - selected[3] / denom, 0.0)
        delta = shrunk - selected[2]
        weights = weights + jnp.dot(pick_hot.T, delta, precision=precise)
        tiles_sel = tiles[chosen]
        rows_sel = row_index[chosen].reshape(-1)
        values = jnp.einsum("bkrf,bf->bkr", tiles_sel, delta, precision=precise).reshape(-1, 128)
        all_values, all_rows = (
            lax.all_gather(values, "feat", axis=0, tiled=True),
            lax.all_gather(rows_sel, "feat", axis=0, tiled=True),
        )
        row_hot = (all_rows[:, None] == jnp.arange(row_blocks, dtype=jnp.int32)[None, :]).astype(
            jnp.float32
        )
        residual = residual + jnp.dot(row_hot.T, all_values, precision=precise)
    return (weights, residual, jnp.stack(gap_list))


def solution(mesh):
    return jax.shard_map(
        shards,
        mesh=mesh,
        in_specs=(
            P("feat", "samp", None, None),
            P("feat", "samp"),
            P("samp", None),
            P("feat", None),
            P(None, "feat"),
        ),
        out_specs=(P("feat", None), P("samp", None), P()),
        check_vma=False,
    )
```

profile of v0, /device:TPU:0, one launch (start us, length us, event | category | flops | bytes accessed | tf_op | source)
XLA Modules:
  0.0 218.6 jit_solution(5991896953948141936)
XLA Ops:
  1.7 1.2 gather_fusion.1
  3.0 1.2 dynamic-slice
  5.1 1.2 gather_fusion.4
  6.7 1.2 gather_fusion.7
  8.2 13.1 %all-reduce.3 = (s32[256]{0:T(256)S(1)}, s32[256]{0:T(256)S(1)}, s32[256]{0:T(256)S(1)}) all-reduce(s32[256]{0:T(256)S(1)} %dynamic-update-slice, s32[256]{0:T(256)S(1)} %dynamic-update-slice.1, s32[256]{0:T(256)S(1)} %dynamic-update-slice.2), channel_id=1, replica_groups=mesh['feat'=8,'samp'=4] {'feat'}, use_global_device_ids=true, to_apply=%add | all-reduce | flops 768 | bytes 6144
  23.6 4.0 %fusion.43 = f32[4,1,128,1]{2,1,3,0:T(1,128)S(1)} fusion(f32[4,16,128,1]{2,3,1,0:T(1,128)S(1)} %bitcast.150, f32[4,16,128,128]{3,2,1,0:T(8,128)} %param.5), kind=kOutput, calls=%fused_computation.115 | convolution fusion | flops 12582912 | bytes 4229120 | tf_op jit(solution)/shard_map/bkrf,bkr->bf/dot_general | solution.py:25
  28.0 5.7 %all-reduce.7 = (f32[1,4,128]{2,1,0:T(4,128)S(1)}, f32[4,128]{1,0:T(4,128)S(1)}) all-reduce(f32[1,4,128]{2,1,0:T(4,128)S(1)} %bitcast.158, f32[4,128]{1,0:T(4,128)S(1)} %bitcast.157), channel_id=1, replica_groups=mesh['feat'=8,'samp'=4] {'samp'}, use_global_device_ids=true, to_apply=%region_2.0 | all-reduce | flops 1024 | bytes 8192 | tf_op jit(solution)/shard_map/psum | solution.py:29
  34.0 2.9 %gather_fusion.2 = f32[2,16,128,128]{3,2,1,0:T(8,128)S(1)} fusion(f32[4,16,128,128]{3,2,1,0:T(8,128)} %param.5, s32[1024]{0:T(1024)S(1)} %pad_clamp_fusion.2), kind=kCustom, calls=%fused_computation.2 | custom fusion | bytes 4194312 | tf_op jit(solution)/shard_map/gather | solution.py:53
  36.9 1.9 fusion.44
  38.8 30.5 %all_gather.19 = f32[256,128]{1,0:T(8,128)S(1)} all-gather(f32[32,128]{1,0:T(8,128)S(1)} %bitcast.153), channel_id=1, replica_groups=mesh['feat'=8,'samp'=4] {'feat'}, dimensions={0}, use_global_device_ids=true | all-gather | bytes 147456 | tf_op jit(solution)/shard_map/all_gather | solution.py:57
  70.6 3.8 %fusion.45 = f32[4,1,128,1]{2,1,3,0:T(1,128)S(1)} fusion(f32[4,16,128,1]{2,3,1,0:T(1,128)S(1)} %bitcast.152, f32[4,16,128,128]{3,2,1,0:T(8,128)} %param.5), kind=kOutput, calls=%fused_computation.117 | convolution fusion | flops 12582912 | bytes 4229120 | tf_op jit(solution)/shard_map/bkrf,bkr->bf/dot_general | solution.py:25
  74.4 5.7 %psum.93 = f32[4,128]{1,0:T(4,128)S(1)} all-reduce(f32[4,128]{1,0:T(4,128)S(1)} %bitcast.159), channel_id=1, replica_groups=mesh['feat'=8,'samp'=4] {'samp'}, use_global_device_ids=true, to_apply=%region_3.0 | all-reduce | flops 512 | bytes 4096 | tf_op jit(solution)/shard_map/psum | solution.py:34
  80.6 2.9 %gather_fusion.5 = f32[2,16,128,128]{3,2,1,0:T(8,128)S(1)} fusion(f32[4,16,128,128]{3,2,1,0:T(8,128)} %param.5, s32[1024]{0:T(1024)S(1)} %pad_clamp_fusion.1), kind=kCustom, calls=%fused_computation.5 | custom fusion | bytes 4194312 | tf_op jit(solution)/shard_map/gather | solution.py:53
  83.5 1.9 fusion.46
  85.3 30.5 %all_gather.21 = f32[256,128]{1,0:T(8,128)S(1)} all-gather(f32[32,128]{1,0:T(8,128)S(1)} %bitcast.154), channel_id=1, replica_groups=mesh['feat'=8,'samp'=4] {'feat'}, dimensions={0}, use_global_device_ids=true | all-gather | bytes 147456 | tf_op jit(solution)/shard_map/all_gather | solution.py:57
  115.9 1.4 multiply_reduce_fusion.5
  117.8 3.8 %fusion.47 = f32[4,1,128,1]{2,1,3,0:T(1,128)S(1)} fusion(f32[4,16,128,1]{2,3,1,0:T(1,128)S(1)} %bitcast.151, f32[4,16,128,128]{3,2,1,0:T(8,128)} %param.5), kind=kOutput, calls=%fused_computation.119 | convolution fusion | flops 12582912 | bytes 4229120 | tf_op jit(solution)/shard_map/bkrf,bkr->bf/dot_general | solution.py:25
  121.7 6.5 %all-reduce.6 = (f32[4,128]{1,0:T(4,128)S(1)}, f32[]{:T(128)}, f32[]{:T(128)}, f32[]{:T(128)}, f32[]{:T(128)}, /*index=5*/f32[]{:T(128)}, f32[]{:T(128)}) all-reduce(f32[4,128]{1,0:T(4,128)S(1)} %bitcast.156, f32[]{:T(128)} %get-tuple-element.6, f32[]{:T(128)} %get-tuple-element.5, ...), channel_id=1, replica_groups=mesh['feat'=8,'samp'=4] {'samp'}, use_global_device_ids=true, to_apply=%region_4.0 | all-reduce | flops 518 | bytes 4144 | tf_op jit(solution)/shard_map/psum | solution.py:34
  129.1 19.3 %all-reduce.5 = (f32[]{:T(128)}, f32[]{:T(128)}, f32[]{:T(128)}) all-reduce(f32[]{:T(128)} %get-tuple-element.13, f32[]{:T(128)} %get-tuple-element.11, f32[]{:T(128)} %get-tuple-element.9), channel_id=1, replica_groups=mesh['feat'=8,'samp'=4] {'feat'}, use_global_device_ids=true, to_apply=%region_26.0 | all-reduce | flops 3 | bytes 24 | tf_op jit(solution)/shard_map/pmin | solution.py:37
  151.6 18.5 %all-reduce.4 = (f32[]{:T(128)}, f32[]{:T(128)}, f32[]{:T(128)}) all-reduce(f32[]{:T(128)} %get-tuple-element.14, f32[]{:T(128)} %get-tuple-element.10, f32[]{:T(128)} %get-tuple-element.12), channel_id=1, replica_groups=mesh['feat'=8,'samp'=4] {'feat'}, use_global_device_ids=true, to_apply=%region_24.0 | all-reduce | flops 3 | bytes 24 | tf_op jit(solution)/shard_map/psum | solution.py:38
  181.1 2.9 %gather_fusion.8 = f32[2,16,128,128]{3,2,1,0:T(8,128)S(1)} fusion(f32[4,16,128,128]{3,2,1,0:T(8,128)} %param.5, s32[1024]{0:T(1024)S(1)} %pad_clamp_fusion), kind=kCustom, calls=%fused_computation.8 | custom fusion | bytes 4194312 | tf_op jit(solution)/shard_map/gather | solution.py:53
  183.9 1.9 fusion.48
  185.8 30.5 %all_gather.23 = f32[256,128]{1,0:T(8,128)S(1)} all-gather(f32[32,128]{1,0:T(8,128)S(1)} %bitcast.155), channel_id=1, replica_groups=mesh['feat'=8,'samp'=4] {'feat'}, dimensions={0}, use_global_device_ids=true | all-gather | bytes 147456 | tf_op jit(solution)/shard_map/all_gather | solution.py:57
  216.3 1.4 convolution_add_fusion
  (41 shorter events, 9.9 us)
Async XLA Ops:
  23.6 4.0 %copy-start = (f32[4,16,128,128]{3,2,1,0:T(8,128)S(1)}, f32[4,16,128,128]{3,2,1,0:T(8,128)}, u32[]{:S(2)}) copy-start(f32[4,16,128,128]{3,2,1,0:T(8,128)} %param.5) | copy-start | bytes 12582916
  27.6 6.1 %copy-start.2 = (f32[4,128]{1,0:T(4,128)S(1)}, f32[4,128]{1,0:T(4,128)}, u32[]{:S(2)}) copy-start(f32[4,128]{1,0:T(4,128)} %param.8) | copy-start | bytes 6148
  36.9 32.4 %copy-start.1 = (f32[512,128]{1,0:T(8,128)S(1)}, f32[512,128]{1,0:T(8,128)}, u32[]{:S(2)}) copy-start(f32[512,128]{1,0:T(8,128)} %param.7) | copy-start | bytes 786436
where the time goes:
time: 219 us
  blocking collectives  160 us (73%)
  matrix products  23.3 us (11%)
  local copies, waits for them, and re-layouts  17.4 us (8%)
  between operations  14.8 us (7%)
  other arithmetic  2.71 us (1%)
    all_gather x3, blocking collectives, shards(): lax.all_gather(values, 'feat', axis=0, tiled=True)  91.6 us
    pmin x1, blocking collectives, shards(): scale = lax.pmin(ratio_local, 'feat')  19.3 us
    psum x1, blocking collectives, shards(): norm_one = lax.psum(norm_local, 'feat')  18.5 us
    unnamed x1, blocking collectives  13.1 us
    psum x2, blocking collectives, shards(): grad, sum_rr, sum_ry = lax.psum((grad_local, rr_local, ry_local), 'samp')  12.1 us
    dot_general x3, matrix products, shards(): grad_local = jnp.einsum('bkrf,bkr->bf', tiles, fetched, precision=precise)  11.7 us
    gather x3, local copies, waits for them, and re-layouts, shards(): tiles_sel = tiles[chosen]  8.63 us
    psum x1, blocking collectives, shards(): lax.psum((grad_local, rr_local, ry_local, col_local), 'samp')  5.67 us

commit v1 on v0

v1 whole, which is shorter than its diff:
```python
import functools

import jax
import jax.numpy as jnp
from jax import lax
from jax.experimental import pallas as pl
from jax.experimental.pallas import tpu as pltpu
from jax.sharding import PartitionSpec as P

STEP_SCALE = 2.0
EPSILON = 1e-06
MESH = pl.DeviceIdType.MESH
UNROLL_PEERS = 8


def each(count, body):
    if count <= UNROLL_PEERS:
        for d in range(1, count):
            body(d)
    else:
        lax.fori_loop(1, count, lambda d, c: (body(d), c)[1], 0)


def split3(v):
    hi = v.astype(jnp.bfloat16)
    rest = v - hi.astype(jnp.float32)
    mid = rest.astype(jnp.bfloat16)
    low = (rest - mid.astype(jnp.float32)).astype(jnp.bfloat16)
    return jnp.concatenate([hi, mid, low], axis=1)


def join3(p):
    w = p.shape[1] // 3
    return p[:, :w] + (p[:, w : 2 * w] + p[:, 2 * w :])


def kernel(
    nf, ns, tiles_hbm, rows_s, targets, penalty, picks,
    weights, residual, gaps,
    tiles_v, tiles_t, fetched, own_rows, rows_all, gbuf, vbuf, stat_f, stat_s,
    delta_buf, colsq, parts, hot_f, hot_r,
    dma_sem, fsend, frecv, ssend, srecv,
):
    iters, batch = picks.shape
    fb, k_tiles = rows_s.shape
    w = tiles_hbm.shape[-1]
    lanes = rows_all.shape[2]
    per = batch * k_tiles
    f_me, s_me = lax.axis_index("feat"), lax.axis_index("samp")
    half = k_tiles // 2

    def tile_copy(b, h):
        return pltpu.make_async_copy(
            tiles_hbm.at[b, pl.ds(h * half, half)],
            tiles_v.at[b, pl.ds(h * half, half)],
            dma_sem.at[b, h],
        )

    for b in range(fb):
        for h in range(2):
            tile_copy(b, h).start()

    barrier = pltpu.get_barrier_semaphore()
    each(nf, lambda d: pl.semaphore_signal(
        barrier, inc=1, device_id={"feat": lax.rem(f_me + d, nf)}, device_id_type=MESH))
    each(ns, lambda d: pl.semaphore_signal(
        barrier, inc=1, device_id={"samp": lax.rem(s_me + d, ns)}, device_id_type=MESH))

    def feat_copy(r, ref, d, slot):
        return pltpu.make_async_remote_copy(
            src_ref=ref.at[slot], dst_ref=ref.at[slot],
            send_sem=fsend.at[r, d], recv_sem=frecv.at[r, slot],
            device_id={"feat": lax.rem(f_me + d, nf)}, device_id_type=MESH)

    def samp_copy(r, ref, d, slot):
        return pltpu.make_async_remote_copy(
            src_ref=ref.at[slot], dst_ref=ref.at[slot],
            send_sem=ssend.at[r, d], recv_sem=srecv.at[r, slot],
            device_id={"samp": lax.rem(s_me + d, ns)}, device_id_type=MESH)

    def feat_send(r, ref):
        each(nf, lambda d: feat_copy(r, ref, d, f_me).start())

    def feat_wait(r, ref):
        each(nf, lambda d: feat_copy(r, ref, d, lax.rem(f_me + d, nf)).wait_recv())

    def samp_send(r, ref):
        each(ns, lambda d: samp_copy(r, ref, d, s_me).start())

    def samp_wait(r, ref):
        each(ns, lambda d: samp_copy(r, ref, d, lax.rem(s_me + d, ns)).wait_recv())

    lane = lax.broadcasted_iota(jnp.int32, (1, lanes), 1)
    for t in range(iters):
        message = jnp.zeros((1, lanes), jnp.int32)
        for i in range(batch):
            p = picks[t, i]
            for k in range(k_tiles):
                message = jnp.where(lane == f_me * per + (i * k_tiles + k), rows_s[p, k], message)
        rows_all[f_me, pl.ds(t, 1), :] = message

    for b in range(fb):
        for k in range(k_tiles):
            row = rows_s[b, k]
            fetched[pl.ds(b * k_tiles + k, 1), :] = -targets[pl.ds(row, 1), :]
            own_rows[pl.ds(b * k_tiles + k, 1), :] = jnp.full((1, w), row, jnp.int32)

    pl.semaphore_wait(barrier, (nf - 1) + (ns - 1))
    feat_send(0, rows_all)

    target = targets[...]
    residual[...] = -target
    square = jnp.sum(target * target, axis=0, keepdims=True)
    stat_s[s_me, pl.ds(0, 1), :] = square
    stat_s[s_me, pl.ds(iters, 1), :] = -square

    g0 = gbuf.at[0]

    def first(b, carry):
        acc = jnp.zeros((w, w), jnp.float32)
        sq = jnp.zeros((8, w), jnp.float32)
        for h in range(2):
            tile_copy(b, h).wait()
            for k in range(h * half, (h + 1) * half):
                tile = tiles_v[b, k]
                turned = tile.T
                tiles_t[b, k] = turned
                acc = acc + turned * fetched[pl.ds(b * k_tiles + k, 1), :]
                sq = sq + jnp.sum((tile * tile).reshape(w // 8, 8, w), axis=0)
        g0[s_me, pl.ds(b, 1), :] = jnp.sum(acc.T, axis=0, keepdims=True)
        g0[s_me, pl.ds(fb + b, 1), :] = jnp.sum(sq, axis=0, keepdims=True)
        return carry

    lax.fori_loop(0, fb, first, 0)
    weights[...] = jnp.zeros_like(weights)

    for t in range(iters):
        gt = gbuf.at[t]
        if t > 0:
            def later(b, carry, gt=gt):
                acc = jnp.zeros((w, w), jnp.float32)
                for k in range(k_tiles):
                    acc = acc + tiles_t[b, k] * fetched[pl.ds(b * k_tiles + k, 1), :]
                gt[s_me, pl.ds(b, 1), :] = jnp.sum(acc.T, axis=0, keepdims=True)
                return carry

            lax.fori_loop(0, fb, later, 0)
        samp_send(t, gt)
        if t > 0:
            residual[...] += join3(jnp.dot(
                hot_r[...], parts[...], preferred_element_type=jnp.float32))
            res = residual[...]
            stat_s[s_me, pl.ds(t, 1), :] = jnp.sum(res * res, axis=0, keepdims=True)
            stat_s[s_me, pl.ds(iters + t, 1), :] = jnp.sum(
                res * targets[...], axis=0, keepdims=True)
        else:
            feat_wait(0, rows_all)
        if t == iters - 1:
            samp_send(iters, stat_s)
        samp_wait(t, gt)
        total = gt[0]
        for s in range(1, ns):
            total = total + gt[s]
        grad = total[:fb]
        if t == 0:
            colsq[...] = total[fb:]
        pen = penalty[...]
        old = weights[...]
        denom = STEP_SCALE * (colsq[...] + EPSILON)
        moved = old - grad / denom
        size = jnp.maximum(jnp.abs(moved) - pen / denom, 0.0)
        block = lax.broadcasted_iota(jnp.int32, (fb, w), 0)
        picked = block == picks[t, 0]
        for i in range(1, batch):
            picked = picked | (block == picks[t, i])
        delta = jnp.where(picked, jnp.where(moved >= 0.0, size, -size) - old, 0.0)
        delta_buf[...] = delta
        vt = vbuf.at[t]
        for i in range(batch):
            p = picks[t, i]
            column = jnp.broadcast_to(delta_buf[pl.ds(p, 1), :], (w, w)).T
            for k in range(k_tiles):
                vt[f_me, pl.ds(i * k_tiles + k, 1), :] = jnp.sum(
                    tiles_t[p, k] * column, axis=0, keepdims=True)
        feat_send(1 + t, vt)
        stat_f[f_me, pl.ds(t, 1), :] = jnp.min(
            pen / jnp.maximum(jnp.abs(grad), pen), axis=0, keepdims=True)
        stat_f[f_me, pl.ds(iters + t, 1), :] = jnp.sum(
            pen * jnp.abs(old), axis=0, keepdims=True)
        weights[...] = old + delta
        if t == iters - 1:
            feat_send(1 + iters, stat_f)
        rows_t = rows_all[0, pl.ds(t, 1), :]
        for f in range(1, nf):
            rows_t = rows_t + rows_all[f, pl.ds(t, 1), :]
        if t < iters - 1:
            own = jnp.concatenate([own_rows[...]] * (lanes // w), axis=1)
            hot_f[...] = jnp.where(own == rows_t, 1.0, 0.0).astype(jnp.bfloat16)
        number = lax.broadcasted_iota(jnp.int32, hot_r.shape, 0)
        hot_r[...] = jnp.where(number == rows_t, 1.0, 0.0).astype(jnp.bfloat16)
        feat_wait(1 + t, vt)
        split = split3(vt[...].reshape(lanes, w))
        if t < iters - 1:
            parts[...] = split
            fetched[...] += join3(jnp.dot(
                hot_f[...], split, preferred_element_type=jnp.float32))
        else:
            residual[...] += join3(jnp.dot(
                hot_r[...], split, preferred_element_type=jnp.float32))

    samp_wait(iters, stat_s)
    feat_wait(1 + iters, stat_f)
    stats = stat_s[0]
    for s in range(1, ns):
        stats = stats + stat_s[s]
    low, norm = stat_f[0], stat_f[0]
    for f in range(1, nf):
        low, norm = jnp.minimum(low, stat_f[f]), norm + stat_f[f]
    rr = jnp.sum(stats[:iters], axis=1, keepdims=True)
    ry = jnp.sum(stats[iters : 2 * iters], axis=1, keepdims=True)
    scale = jnp.min(low[:iters], axis=1, keepdims=True)
    norm_one = jnp.sum(norm[iters : 2 * iters], axis=1, keepdims=True)
    value = (0.5 * rr + norm_one + 0.5 * scale * scale * rr + scale * ry) / (0.5 * rr[0:1])
    for t in range(iters):
        gaps[t] = jnp.sum(value[t : t + 1])

    def drain_feat(d):
        feat_copy(0, rows_all, d, f_me).wait_send()
        for t in range(iters):
            feat_copy(1 + t, vbuf.at[t], d, f_me).wait_send()
        feat_copy(1 + iters, stat_f, d, f_me).wait_send()

    def drain_samp(d):
        for t in range(iters):
            samp_copy(t, gbuf.at[t], d, s_me).wait_send()
        samp_copy(iters, stat_s, d, s_me).wait_send()

    each(nf, drain_feat)
    each(ns, drain_samp)


def solution(mesh):
    nf, ns = mesh.shape["feat"], mesh.shape["samp"]

    def shards(tiles, row_index, targets, penalty, picks):
        fb, k_tiles, w, _ = tiles.shape
        iters, batch = picks.shape
        rb = targets.shape[0]
        per = batch * k_tiles
        lanes = nf * per
        stat_rows = -(-2 * iters // 8) * 8
        vmem, smem = pltpu.VMEM, pltpu.SMEM
        f32, i32 = jnp.float32, jnp.int32
        spec = lambda space: pl.BlockSpec(memory_space=space)
        return pl.pallas_call(
            functools.partial(kernel, nf, ns),
            out_shape=(
                jax.ShapeDtypeStruct((fb, w), f32),
                jax.ShapeDtypeStruct((rb, w), f32),
                jax.ShapeDtypeStruct((iters,), f32),
            ),
            in_specs=[spec(pl.ANY), spec(smem), spec(vmem), spec(vmem), spec(smem)],
            out_specs=(spec(vmem), spec(vmem), spec(smem)),
            scratch_shapes=[
                vmem((fb, k_tiles, w, w), f32),
                vmem((fb, k_tiles, w, w), f32),
                vmem((fb * k_tiles, w), f32),
                vmem((fb * k_tiles, w), i32),
                vmem((nf, -(-iters // 8) * 8, lanes), i32),
                vmem((iters, ns, 2 * fb, w), f32),
                vmem((iters, nf, per, w), f32),
                vmem((nf, stat_rows, w), f32),
                vmem((ns, stat_rows, w), f32),
                vmem((fb, w), f32),
                vmem((fb, w), f32),
                vmem((lanes, 3 * w), jnp.bfloat16),
                vmem((fb * k_tiles, lanes), jnp.bfloat16),
                vmem((rb, lanes), jnp.bfloat16),
                pltpu.SemaphoreType.DMA((fb, 2)),
                pltpu.SemaphoreType.DMA((iters + 2, nf)),
                pltpu.SemaphoreType.DMA((iters + 2, nf)),
                pltpu.SemaphoreType.DMA((iters + 1, ns)),
                pltpu.SemaphoreType.DMA((iters + 1, ns)),
            ],
            compiler_params=pltpu.CompilerParams(collective_id=0, has_side_effects=True),
        )(tiles, row_index, targets, penalty, picks)

    return jax.shard_map(
        shards,
        mesh=mesh,
        in_specs=(
            P("feat", "samp", None, None),
            P("feat", "samp"),
            P("samp", None),
            P("feat", None),
            P(None, "feat"),
        ),
        out_specs=(P("feat", None), P("samp", None), P()),
        check_vma=False,
    )
```

time: 219 us -> 43.8 us (0.20)
  blocking collectives: 160 us -> 0 us
  Pallas kernels: 0 us -> 37.6 us
  matrix products: 23.3 us -> 0 us
  between operations: 14.8 us -> 0.64 us
  local copies, waits for them, and re-layouts: 17.4 us -> 5.34 us
  other arithmetic: 2.71 us -> 0 us
    all_gather x3 -> x0, blocking collectives: 91.6 us -> none  [shards(): lax.all_gather(values, 'feat', axis=0, tiled=True)]
    pallas_call x0 -> x1, Pallas kernels: none -> 37.6 us  [shards(): pl.pallas_call(functools.partial(kernel, nf, ns), out_shape=(jax.ShapeDty...]
    psum x4 -> x0, blocking collectives: 36.4 us -> none  [the longest x1 18.5 us: shards(): norm_one = lax.psum(norm_local, 'feat')]
    dot_general x15 -> x0, matrix products: 23.3 us -> none  [the longest x3 11.7 us: shards(): grad_local = jnp.einsum('bkrf,bkr->bf', tiles, fetched, precision=precise)]
    pmin x1 -> x0, blocking collectives: 19.3 us -> none  [shards(): scale = lax.pmin(ratio_local, 'feat')]
    gather x9 -> x0, local copies, waits for them, and re-layouts: 14.2 us -> none  [the longest x3 8.63 us: shards(): tiles_sel = tiles[chosen]]
    unnamed x1 -> x0, blocking collectives: 13.1 us -> none
    unnamed x13 -> x4, local copies, waits for them, and re-layouts: 1.87 us -> 5.34 us
where the time goes in v1:
time: 43.8 us; the launch traced here: 43.6 us
  Pallas kernels  37.6 us (86%)
  local copies, waits for them, and re-layouts  5.34 us (12%)
  between operations  0.64 us (1%)
    pallas_call x1, Pallas kernels, shards(): pl.pallas_call(functools.partial(kernel, nf, ns), out_shape=(jax.ShapeDty...  37.6 us
    unnamed x4, local copies, waits for them, and re-layouts  5.34 us

profile of v1, /device:TPU:0, one launch (start us, length us, event | category | flops | bytes accessed | tf_op | source)
XLA Modules:
  0.0 43.6 jit_solution(7518204755822063271)
XLA Ops:
  0.6 1.3 %copy.8.picks = s32[3,2]{1,0:T(4,128)} copy(s32[3,2]{0,1:T(2,128)} %param.9) | data formatting | bytes 48 | tf_op args[4]
  2.0 37.6 %shard_map.76 = (f32[4,128]{1,0:T(4,128)}, f32[512,128]{1,0:T(8,128)}, f32[3]{0:T(128)}) custom-call(f32[4,16,128,128]{3,2,1,0:T(8,128)} %tiles_hbm.1, s32[4,16]{1,0:T(4,128)} %rows_s.1, f32[512,128]{1,0:T(8,128)} %targets.1, f32[4,128]{1,0:T(4,128)} %penalty.1, s32[3,2]{1,0:T(4,128)} %copy.8.picks), custom_call_target="tpu_custom_call" | custom-call | tf_op jit(solution)/shard_map/pallas_call | solution.py:255
  39.6 1.2 %copy.12 = f32[4,128]{1,0:T(4,128)} copy(f32[4,128]{1,0:T(4,128)} %get-tuple-element.6) | data formatting | bytes 4096
  40.8 1.7 %copy.13 = f32[512,128]{1,0:T(8,128)} copy(f32[512,128]{1,0:T(8,128)} %get-tuple-element.7) | data formatting | bytes 524288
  42.5 1.1 %copy.14 = f32[3]{0:T(128)} copy(f32[3]{0:T(128)} %get-tuple-element.8) | data formatting | bytes 24

commit v2 on v1

--- a/solution.py
+++ b/solution.py
@@ -15,10 +15,21 @@
 
 def each(count, body):
     if count <= UNROLL_PEERS:
-        for d in range(1, count):
+        for d in range(count - 1, 0, -1):
             body(d)
     else:
         lax.fori_loop(1, count, lambda d, c: (body(d), c)[1], 0)
+
+
+def partner(me, d, count):
+    if not isinstance(d, int) or count & (count - 1):
+        return lax.rem(me + d, count)
+    other, bit = 0, 1
+    while bit < count:
+        v = lax.rem(lax.div(me, bit), 2)
+        other = other + bit * (1 - v if d & bit else v)
+        bit *= 2
+    return other
 
 
 def split3(v):
@@ -35,13 +46,13 @@
 
 
 def kernel(
-    nf, ns, tiles_hbm, rows_s, targets, penalty, picks,
+    nf, ns, tiles_hbm, rows_hbm, targets_hbm, penalty_hbm, picks_hbm,
     weights, residual, gaps,
-    tiles_v, tiles_t, fetched, own_rows, rows_all, gbuf, vbuf, stat_f, stat_s,
+    rows_s, picks, targets, penalty, tiles_v, tiles_t, fetched, own_rows, rows_all, gbuf, vbuf, stat_f, stat_s,
     delta_buf, colsq, parts, hot_f, hot_r,
-    dma_sem, fsend, frecv, ssend, srecv,
+    in_sem, dma_sem, fsend, frecv, ssend, srecv,
 ):
-    iters, batch = picks.shape
+    batch, iters = picks.shape
     fb, k_tiles = rows_s.shape
     w = tiles_hbm.shape[-1]
     lanes = rows_all.shape[2]
@@ -56,57 +67,66 @@
             dma_sem.at[b, h],
         )
 
+    small = [
+        pltpu.make_async_copy(src, dst, in_sem.at[n])
+        for n, (src, dst) in enumerate((
+            (rows_hbm, rows_s), (picks_hbm, picks), (targets_hbm, targets), (penalty_hbm, penalty)))
+    ]
+    for copy in small:
+        copy.start()
     for b in range(fb):
         for h in range(2):
             tile_copy(b, h).start()
 
     barrier = pltpu.get_barrier_semaphore()
     each(nf, lambda d: pl.semaphore_signal(
-        barrier, inc=1, device_id={"feat": lax.rem(f_me + d, nf)}, device_id_type=MESH))
+        barrier, inc=1, device_id={"feat": partner(f_me, d, nf)}, device_id_type=MESH))
     each(ns, lambda d: pl.semaphore_signal(
-        barrier, inc=1, device_id={"samp": lax.rem(s_me + d, ns)}, device_id_type=MESH))
+        barrier, inc=1, device_id={"samp": partner(s_me, d, ns)}, device_id_type=MESH))
 
     def feat_copy(r, ref, d, slot):
         return pltpu.make_async_remote_copy(
             src_ref=ref.at[slot], dst_ref=ref.at[slot],
             send_sem=fsend.at[r, d], recv_sem=frecv.at[r, slot],
-            device_id={"feat": lax.rem(f_me + d, nf)}, device_id_type=MESH)
+            device_id={"feat": partner(f_me, d, nf)}, device_id_type=MESH)
 
     def samp_copy(r, ref, d, slot):
         return pltpu.make_async_remote_copy(
             src_ref=ref.at[slot], dst_ref=ref.at[slot],
             send_sem=ssend.at[r, d], recv_sem=srecv.at[r, slot],
-            device_id={"samp": lax.rem(s_me + d, ns)}, device_id_type=MESH)
+            device_id={"samp": partner(s_me, d, ns)}, device_id_type=MESH)
 
     def feat_send(r, ref):
         each(nf, lambda d: feat_copy(r, ref, d, f_me).start())
 
     def feat_wait(r, ref):
-        each(nf, lambda d: feat_copy(r, ref, d, lax.rem(f_me + d, nf)).wait_recv())
+        each(nf, lambda d: feat_copy(r, ref, d, partner(f_me, d, nf)).wait_recv())
 
     def samp_send(r, ref):
         each(ns, lambda d: samp_copy(r, ref, d, s_me).start())
 
     def samp_wait(r, ref):
-        each(ns, lambda d: samp_copy(r, ref, d, lax.rem(s_me + d, ns)).wait_recv())
+        each(ns, lambda d: samp_copy(r, ref, d, partner(s_me, d, ns)).wait_recv())
+
+    small[0].wait()
+    small[1].wait()
 
     lane = lax.broadcasted_iota(jnp.int32, (1, lanes), 1)
     for t in range(iters):
         message = jnp.zeros((1, lanes), jnp.int32)
         for i in range(batch):
-            p = picks[t, i]
+            p = picks[i, t]
             for k in range(k_tiles):
                 message = jnp.where(lane == f_me * per + (i * k_tiles + k), rows_s[p, k], message)
         rows_all[f_me, pl.ds(t, 1), :] = message
 
+    small[2].wait()
+    small[3].wait()
     for b in range(fb):
         for k in range(k_tiles):
             row = rows_s[b, k]
             fetched[pl.ds(b * k_tiles + k, 1), :] = -targets[pl.ds(row, 1), :]
             own_rows[pl.ds(b * k_tiles + k, 1), :] = jnp.full((1, w), row, jnp.int32)
-
-    pl.semaphore_wait(barrier, (nf - 1) + (ns - 1))
-    feat_send(0, rows_all)
 
     target = targets[...]
     residual[...] = -target
@@ -145,7 +165,11 @@
                 return carry
 
             lax.fori_loop(0, fb, later, 0)
+        if t == 0:
+            pl.semaphore_wait(barrier, (nf - 1) + (ns - 1))
         samp_send(t, gt)
+        if t == 0:
+            feat_send(0, rows_all)
         if t > 0:
             residual[...] += join3(jnp.dot(
                 hot_r[...], parts[...], preferred_element_type=jnp.float32))
@@ -153,8 +177,6 @@
             stat_s[s_me, pl.ds(t, 1), :] = jnp.sum(res * res, axis=0, keepdims=True)
             stat_s[s_me, pl.ds(iters + t, 1), :] = jnp.sum(
                 res * targets[...], axis=0, keepdims=True)
-        else:
-            feat_wait(0, rows_all)
         if t == iters - 1:
             samp_send(iters, stat_s)
         samp_wait(t, gt)
@@ -170,14 +192,14 @@
         moved = old - grad / denom
         size = jnp.maximum(jnp.abs(moved) - pen / denom, 0.0)
         block = lax.broadcasted_iota(jnp.int32, (fb, w), 0)
-        picked = block == picks[t, 0]
+        picked = block == picks[0, t]
         for i in range(1, batch):
-            picked = picked | (block == picks[t, i])
+            picked = picked | (block == picks[i, t])
         delta = jnp.where(picked, jnp.where(moved >= 0.0, size, -size) - old, 0.0)
         delta_buf[...] = delta
         vt = vbuf.at[t]
         for i in range(batch):
-            p = picks[t, i]
+            p = picks[i, t]
             column = jnp.broadcast_to(delta_buf[pl.ds(p, 1), :], (w, w)).T
             for k in range(k_tiles):
                 vt[f_me, pl.ds(i * k_tiles + k, 1), :] = jnp.sum(
@@ -190,6 +212,8 @@
         weights[...] = old + delta
         if t == iters - 1:
             feat_send(1 + iters, stat_f)
+        if t == 0:
+            feat_wait(0, rows_all)
         rows_t = rows_all[0, pl.ds(t, 1), :]
         for f in range(1, nf):
             rows_t = rows_t + rows_all[f, pl.ds(t, 1), :]
@@ -221,8 +245,7 @@
     scale = jnp.min(low[:iters], axis=1, keepdims=True)
     norm_one = jnp.sum(norm[iters : 2 * iters], axis=1, keepdims=True)
     value = (0.5 * rr + norm_one + 0.5 * scale * scale * rr + scale * ry) / (0.5 * rr[0:1])
-    for t in range(iters):
-        gaps[t] = jnp.sum(value[t : t + 1])
+    gaps[...] = jnp.broadcast_to(value, gaps.shape)
 
     def drain_feat(d):
         feat_copy(0, rows_all, d, f_me).wait_send()
@@ -239,12 +262,26 @@
     each(ns, drain_samp)
 
 
+def hand_out(weights_v, residual_v, gaps_v, weights, residual, gaps, sems):
+    copies = [
+        pltpu.make_async_copy(residual_v, residual, sems.at[0]),
+        pltpu.make_async_copy(weights_v, weights, sems.at[1]),
+    ]
+    for copy in copies:
+        copy.start()
+    for t in range(gaps.shape[0]):
+        gaps[t] = jnp.max(gaps_v[t : t + 1, :])
+    for copy in copies:
+        copy.wait()
+
+
 def solution(mesh):
     nf, ns = mesh.shape["feat"], mesh.shape["samp"]
 
     def shards(tiles, row_index, targets, penalty, picks):
         fb, k_tiles, w, _ = tiles.shape
-        iters, batch = picks.shape
+        picks = picks.T
+        batch, iters = picks.shape
         rb = targets.shape[0]
         per = batch * k_tiles
         lanes = nf * per
@@ -252,16 +289,16 @@
         vmem, smem = pltpu.VMEM, pltpu.SMEM
         f32, i32 = jnp.float32, jnp.int32
         spec = lambda space: pl.BlockSpec(memory_space=space)
-        return pl.pallas_call(
+        done = pl.pallas_call(
             functools.partial(kernel, nf, ns),
-            out_shape=(
-                jax.ShapeDtypeStruct((fb, w), f32),
-                jax.ShapeDtypeStruct((rb, w), f32),
-                jax.ShapeDtypeStruct((iters,), f32),
-            ),
-            in_specs=[spec(pl.ANY), spec(smem), spec(vmem), spec(vmem), spec(smem)],
-            out_specs=(spec(vmem), spec(vmem), spec(smem)),
+            out_shape=(vmem((fb, w), f32), vmem((rb, w), f32), vmem((iters, w), f32)),
+            in_specs=[spec(pltpu.HBM)] * 5,
+            out_specs=(spec(vmem),) * 3,
             scratch_shapes=[
+                smem((fb, k_tiles), i32),
+                smem((batch, iters), i32),
+                vmem((rb, w), f32),
+                vmem((fb, w), f32),
                 vmem((fb, k_tiles, w, w), f32),
                 vmem((fb, k_tiles, w, w), f32),
                 vmem((fb * k_tiles, w), f32),
@@ -276,14 +313,29 @@
                 vmem((lanes, 3 * w), jnp.bfloat16),
                 vmem((fb * k_tiles, lanes), jnp.bfloat16),
                 vmem((rb, lanes), jnp.bfloat16),
+                pltpu.SemaphoreType.DMA((4,)),
                 pltpu.SemaphoreType.DMA((fb, 2)),
                 pltpu.SemaphoreType.DMA((iters + 2, nf)),
                 pltpu.SemaphoreType.DMA((iters + 2, nf)),
                 pltpu.SemaphoreType.DMA((iters + 1, ns)),
                 pltpu.SemaphoreType.DMA((iters + 1, ns)),
             ],
-            compiler_params=pltpu.CompilerParams(collective_id=0, has_side_effects=True),
-        )(tiles, row_index, targets, penalty, picks)
+            compiler_params=pltpu.CompilerParams(
+                collective_id=0, has_side_effects=True, vmem_limit_bytes=24 * 1024 * 1024),
+        )(*(pltpu.with_memory_space_constraint(a, pltpu.HBM)
+            for a in (tiles, row_index, targets, penalty, picks)))
+        return pl.pallas_call(
+            hand_out,
+            out_shape=(
+                jax.ShapeDtypeStruct((fb, w), f32),
+                jax.ShapeDtypeStruct((rb, w), f32),
+                jax.ShapeDtypeStruct((iters,), f32),
+            ),
+            in_specs=[spec(vmem)] * 3,
+            out_specs=(spec(pltpu.HBM), spec(pltpu.HBM), spec(smem)),
+            scratch_shapes=[pltpu.SemaphoreType.DMA((2,))],
+            compiler_params=pltpu.CompilerParams(vmem_limit_bytes=4 * 1024 * 1024),
+        )(*(pltpu.with_memory_space_constraint(a, pltpu.VMEM) for a in done))
 
     return jax.shard_map(
         shards,

time: 43.8 us -> 37 us (0.84)
  local copies, waits for them, and re-layouts: 5.34 us -> 0 us
  Pallas kernels: 37.6 us -> 36.2 us
    unnamed x4 -> x0, local copies, waits for them, and re-layouts: 5.34 us -> none
    pallas_call x1 -> x2, Pallas kernels: 37.6 us -> 36.2 us  [the longest x1 34.9 us: shards(): pl.pallas_call(functools.partial(kernel, nf, ns), out_shape=(vmem((fb, w)...]
where the time goes in v2:
time: 37 us; the launch traced here: 36.8 us
  Pallas kernels  36.2 us (98%)
  between operations  0.64 us (2%)
    pallas_call x1, Pallas kernels, shards(): pl.pallas_call(functools.partial(kernel, nf, ns), out_shape=(vmem((fb, w)...  34.9 us
    pallas_call x1, Pallas kernels, shards(): pl.pallas_call(hand_out, out_shape=(jax.ShapeDtypeStruct((fb, w), f32), j...  1.24 us

profile of v2, /device:TPU:0, one launch (start us, length us, event | category | flops | bytes accessed | tf_op | source)
XLA Modules:
  0.0 36.8 jit_solution(5953792716304480297)
XLA Ops:
  0.6 34.9 %shard_map.76 = (f32[4,128]{1,0:T(4,128)S(1)}, f32[512,128]{1,0:T(8,128)S(1)}, f32[3,128]{1,0:T(4,128)S(1)}) custom-call(f32[4,16,128,128]{3,2,1,0:T(8,128)} %tiles_hbm.1, s32[4,16]{1,0:T(4,128)} %rows_hbm.1, f32[512,128]{1,0:T(8,128)} %targets_hbm.1, f32[4,128]{1,0:T(4,128)} %penalty_hbm.1, s32[2,3]{1,0:T(2,128)} %bitcast.1), custom_call_target="tpu_custom_call" | custom-call | tf_op jit(solution)/shard_map/pallas_call | solution.py:292
  35.6 1.2 %shard_map.77 = (f32[4,128]{1,0:T(4,128)}, f32[512,128]{1,0:T(8,128)}, f32[3]{0:T(128)}) custom-call(f32[4,128]{1,0:T(4,128)S(1)} %get-tuple-element.6.weights_v, f32[512,128]{1,0:T(8,128)S(1)} %get-tuple-element.7.residual_v, f32[3,128]{1,0:T(4,128)S(1)} %get-tuple-element.8.gaps_v), custom_call_target="tpu_custom_call" | custom-call | tf_op jit(solution)/shard_map/pallas_call | solution.py:327
